TPU v7x, 32 devices: a 4x2x2 block of a 4x4x8 slice. The times are simulated.
32 devices in a mesh: dp: 4 (over y, z), ep: 8 (over x, core).
Axes of the slice: x: 4, y: 2, z: 2, core: 2. Of those that a mesh axis runs over, the one named last changes fastest.
The devices are a block of a 4x4x8 slice.
Arguments:
- x: bfloat16 [16384, 4096], P(('dp', 'ep')), parts along dimension 0
- route_idx: int32 [16384, 2], P(('dp', 'ep')), parts along dimension 0
- gates: float32 [16384, 2], P(('dp', 'ep')), parts along dimension 0
- w1: bfloat16 [8, 4096, 6400], P('ep')
- w3: bfloat16 [8, 4096, 6400], P('ep')
- w2: bfloat16 [8, 6400, 4096], P('ep')
Outputs:
- output: bfloat16 [16384, 4096], P(('dp', 'ep')), parts along dimension 0
There are 4 independent parts. A program takes and returns all parts, laid end to end along the dimension named above; an argument that names none is the same for every part.
All inputs are finite; a program needn't handle non-finite values.
Results may differ from a plain program's by a relative error of at most 0.001.
Values are sent between devices in bfloat16 or wider.
A program may use at most 768 MiB of HBM per device.

v0:
```python
import jax
import jax.numpy as jnp
from jax import lax
from jax.sharding import PartitionSpec as P


def pair_slots(ne, e):
    n = e.shape[0]
    oh = (e[:, :, None] == jnp.arange(ne, dtype=e.dtype)).astype(jnp.float32)
    i = jnp.arange(n, dtype=jnp.int32)
    low = (i[None, :] < i[:, None]).astype(jnp.bfloat16)
    before = jnp.dot(low, jnp.sum(oh, axis=1).astype(jnp.bfloat16), preferred_element_type=jnp.float32)
    return jnp.sum(before[:, None, :] * oh, axis=2).astype(jnp.int32)


def dispatch(x, dest, nrows):
    r = jnp.arange(nrows, dtype=dest.dtype)[:, None]
    p = (dest[None, :, 0] == r) | (dest[None, :, 1] == r)
    return jnp.dot(p.astype(x.dtype), x)


def combine(back, dest, gates):
    r = jnp.arange(back.shape[0], dtype=dest.dtype)[None, :]
    o0 = jnp.dot((dest[:, 0:1] == r).astype(back.dtype), back, preferred_element_type=jnp.float32)
    o1 = jnp.dot((dest[:, 1:2] == r).astype(back.dtype), back, preferred_element_type=jnp.float32)
    return (gates[:, 0:1] * o0 + gates[:, 1:2] * o1).astype(jnp.bfloat16)


def expert_rows(rows, w1, w3, w2):
    a = jnp.dot(rows, w1, preferred_element_type=jnp.float32)
    b = jnp.dot(rows, w3, preferred_element_type=jnp.float32)
    h = (jax.nn.silu(a) * b).astype(jnp.bfloat16)
    return jnp.dot(h, w2, preferred_element_type=jnp.float32).astype(jnp.bfloat16)


def solution(mesh):
    ep = mesh.shape['ep']

    def local(x, route_idx, gates, w1, w3, w2):
        tok, d = x.shape
        cap = 3 * tok // 4
        dest = route_idx * cap + pair_slots(ep, route_idx)
        send = dispatch(x, dest, ep * cap).reshape(ep, cap, d)
        recv = lax.all_to_all(send, 'ep', 0, 0, tiled=True)
        out = lax.map(lambda rows: expert_rows(rows, w1[0], w3[0], w2[0]), recv)
        back = lax.all_to_all(out, 'ep', 0, 0, tiled=True)
        return combine(back.reshape(ep * cap, d), dest, gates)

    spec = P(('dp', 'ep'), None)
    wspec = P('ep', None, None)
    return jax.shard_map(local, mesh=mesh, in_specs=(spec, spec, spec, wspec, wspec, wspec),
                         out_specs=spec, check_vma=False)
```

profile of v0, /device:TPU:81, one launch (start us, length us, event | category | flops | bytes accessed | tf_op | source)
XLA Modules:
  0.0 1350.9 jit_solution(11340842437123439843)
XLA Ops:
  0.0 0.7 convert_reduce_fusion
  0.7 0.2 fusion.48
  0.9 0.7 select_reduce_fusion
  1.7 0.7 convert_add_fusion
  2.4 0.0 copy-start.1
  2.4 0.0 copy-start.3
  2.4 19.0 %fusion.42 = bf16[3072,4096]{1,0:T(8,128)(2,1)} fusion(bf16[512,4096]{1,0:T(8,128)(2,1)} %param.8, s32[512]{0:T(512)S(1)} %bitcast.71, s32[512]{0:T(512)S(1)} %bitcast.73), kind=kOutput, calls=%fused_computation.26 | convolution fusion | flops 12889620480 | bytes 29364224 | tf_op jit(solution)/shard_map/dot_general | solution.py:19
  21.4 0.0 copy-done.1
  21.4 0.0 copy-done.3
  21.4 8.3 all-to-all-start
  29.7 273.4 %all-to-all-done = bf16[8,384,4096]{2,1,0:T(8,128)(2,1)} async-done(((bf16[8,384,4096]{2,1,0:T(8,128)(2,1)}), bf16[8,384,4096]{2,1,0:T(8,128)(2,1)}, u32[]{:S(2)}, u32[]{:S(2)}) %all-to-all-start) | async-done | bytes 25165856 | tf_op jit(solution)/shard_map/all_to_all | solution.py:44
  303.1 726.3 %while.10 = (s32[]{:T(128)}, bf16[8,384,4096]{2,1,0:T(8,128)(2,1)}, bf16[8,384,4096]{2,1,0:T(8,128)(2,1)}, bf16[1,4096,6400]{2,1,0:T(8,128)(2,1)}, bf16[1,4096,6...) while((s32[]{:T(128)}, bf16[8,384,4096]{2,1,0:T(8,128)(2,1)}, ...), condition=%wide.region_3.4_spmd, body=%wide.region_2.3_spmd.sunk | while | flops 60414296064 | bytes 196216400 | solution.py:45
  303.1 31.1 %fusion.78 = f32[384,6400]{1,0:T(8,128)} fusion(bf16[1,4096,6400]{2,1,0:T(8,128)(2,1)} %get-tuple-element.108, bf16[8,384,4096]{2,1,0:T(8,128)(2,1)} %get-tuple-element.107, s32[]{:T(128)} %get-tuple-element.98), kind=kOutput, calls=%fused_computation.4.clone.1 | convolution fusion | flops 20132659200 | bytes 65405440 | tf_op jit(solution)/shard_map/while/body/eval_jaxpr/dot_general | solution.py:30
  334.2 31.6 %fusion.9.clone.12 = bf16[384,6400]{1,0:T(8,128)(2,1)} fusion(bf16[1,4096,6400]{2,1,0:T(8,128)(2,1)} %get-tuple-element.109, f32[384,6400]{1,0:T(8,128)} %fusion.78, bf16[8,384,4096]{2,1,0:T(8,128)(2,1)} %get-tuple-element.107, s32[]{:T(128)} %get-tuple-element.98), kind=kOutput, calls=%fused_computation.7.clone.clone.clone.clone.clone.clone.clone.clone.clone.1.clone.1 | convolution fusion | flops 20147404800 | bytes 70320640 | tf_op jit(solution)/shard_map/while/body/eval_jaxpr/dot_general | solution.py:31
  365.8 28.0 %fusion.79 = bf16[8,384,4096]{2,1,0:T(8,128)(2,1)} fusion(bf16[8,384,4096]{2,1,0:T(8,128)(2,1)} %get-tuple-element.99, s32[]{:T(128)} %get-tuple-element.98, bf16[1,6400,4096]{2,1,0:T(8,128)(2,1)} %get-tuple-element.110, bf16[384,6400]{1,0:T(8,128)(2,1)} %fusion.9.clone.12), kind=kOutput, calls=%fused_computation.10.clone.2 | convolution fusion | flops 20134232064 | bytes 60490240 | tf_op jit(solution)/shard_map/while/body/eval_jaxpr/dot_general | solution.py:33
  393.8 31.1 %fusion.78 = f32[384,6400]{1,0:T(8,128)} fusion(bf16[1,4096,6400]{2,1,0:T(8,128)(2,1)} %get-tuple-element.108, bf16[8,384,4096]{2,1,0:T(8,128)(2,1)} %get-tuple-element.107, s32[]{:T(128)} %get-tuple-element.98), kind=kOutput, calls=%fused_computation.4.clone.1 | convolution fusion | flops 20132659200 | bytes 65405440 | tf_op jit(solution)/shard_map/while/body/eval_jaxpr/dot_general | solution.py:30
  424.9 31.6 %fusion.9.clone.12 = bf16[384,6400]{1,0:T(8,128)(2,1)} fusion(bf16[1,4096,6400]{2,1,0:T(8,128)(2,1)} %get-tuple-element.109, f32[384,6400]{1,0:T(8,128)} %fusion.78, bf16[8,384,4096]{2,1,0:T(8,128)(2,1)} %get-tuple-element.107, s32[]{:T(128)} %get-tuple-element.98), kind=kOutput, calls=%fused_computation.7.clone.clone.clone.clone.clone.clone.clone.clone.clone.1.clone.1 | convolution fusion | flops 20147404800 | bytes 70320640 | tf_op jit(solution)/shard_map/while/body/eval_jaxpr/dot_general | solution.py:31
  456.6 28.0 %fusion.79 = bf16[8,384,4096]{2,1,0:T(8,128)(2,1)} fusion(bf16[8,384,4096]{2,1,0:T(8,128)(2,1)} %get-tuple-element.99, s32[]{:T(128)} %get-tuple-element.98, bf16[1,6400,4096]{2,1,0:T(8,128)(2,1)} %get-tuple-element.110, bf16[384,6400]{1,0:T(8,128)(2,1)} %fusion.9.clone.12), kind=kOutput, calls=%fused_computation.10.clone.2 | convolution fusion | flops 20134232064 | bytes 60490240 | tf_op jit(solution)/shard_map/while/body/eval_jaxpr/dot_general | solution.py:33
  484.6 31.1 %fusion.78 = f32[384,6400]{1,0:T(8,128)} fusion(bf16[1,4096,6400]{2,1,0:T(8,128)(2,1)} %get-tuple-element.108, bf16[8,384,4096]{2,1,0:T(8,128)(2,1)} %get-tuple-element.107, s32[]{:T(128)} %get-tuple-element.98), kind=kOutput, calls=%fused_computation.4.clone.1 | convolution fusion | flops 20132659200 | bytes 65405440 | tf_op jit(solution)/shard_map/while/body/eval_jaxpr/dot_general | solution.py:30
  515.7 31.6 %fusion.9.clone.12 = bf16[384,6400]{1,0:T(8,128)(2,1)} fusion(bf16[1,4096,6400]{2,1,0:T(8,128)(2,1)} %get-tuple-element.109, f32[384,6400]{1,0:T(8,128)} %fusion.78, bf16[8,384,4096]{2,1,0:T(8,128)(2,1)} %get-tuple-element.107, s32[]{:T(128)} %get-tuple-element.98), kind=kOutput, calls=%fused_computation.7.clone.clone.clone.clone.clone.clone.clone.clone.clone.1.clone.1 | convolution fusion | flops 20147404800 | bytes 70320640 | tf_op jit(solution)/shard_map/while/body/eval_jaxpr/dot_general | solution.py:31
  547.3 28.0 %fusion.79 = bf16[8,384,4096]{2,1,0:T(8,128)(2,1)} fusion(bf16[8,384,4096]{2,1,0:T(8,128)(2,1)} %get-tuple-element.99, s32[]{:T(128)} %get-tuple-element.98, bf16[1,6400,4096]{2,1,0:T(8,128)(2,1)} %get-tuple-element.110, bf16[384,6400]{1,0:T(8,128)(2,1)} %fusion.9.clone.12), kind=kOutput, calls=%fused_computation.10.clone.2 | convolution fusion | flops 20134232064 | bytes 60490240 | tf_op jit(solution)/shard_map/while/body/eval_jaxpr/dot_general | solution.py:33
  575.4 31.1 %fusion.78 = f32[384,6400]{1,0:T(8,128)} fusion(bf16[1,4096,6400]{2,1,0:T(8,128)(2,1)} %get-tuple-element.108, bf16[8,384,4096]{2,1,0:T(8,128)(2,1)} %get-tuple-element.107, s32[]{:T(128)} %get-tuple-element.98), kind=kOutput, calls=%fused_computation.4.clone.1 | convolution fusion | flops 20132659200 | bytes 65405440 | tf_op jit(solution)/shard_map/while/body/eval_jaxpr/dot_general | solution.py:30
  606.5 31.6 %fusion.9.clone.12 = bf16[384,6400]{1,0:T(8,128)(2,1)} fusion(bf16[1,4096,6400]{2,1,0:T(8,128)(2,1)} %get-tuple-element.109, f32[384,6400]{1,0:T(8,128)} %fusion.78, bf16[8,384,4096]{2,1,0:T(8,128)(2,1)} %get-tuple-element.107, s32[]{:T(128)} %get-tuple-element.98), kind=kOutput, calls=%fused_computation.7.clone.clone.clone.clone.clone.clone.clone.clone.clone.1.clone.1 | convolution fusion | flops 20147404800 | bytes 70320640 | tf_op jit(solution)/shard_map/while/body/eval_jaxpr/dot_general | solution.py:31
  638.1 28.0 %fusion.79 = bf16[8,384,4096]{2,1,0:T(8,128)(2,1)} fusion(bf16[8,384,4096]{2,1,0:T(8,128)(2,1)} %get-tuple-element.99, s32[]{:T(128)} %get-tuple-element.98, bf16[1,6400,4096]{2,1,0:T(8,128)(2,1)} %get-tuple-element.110, bf16[384,6400]{1,0:T(8,128)(2,1)} %fusion.9.clone.12), kind=kOutput, calls=%fused_computation.10.clone.2 | convolution fusion | flops 20134232064 | bytes 60490240 | tf_op jit(solution)/shard_map/while/body/eval_jaxpr/dot_general | solution.py:33
  666.1 31.2 %fusion.78 = f32[384,6400]{1,0:T(8,128)} fusion(bf16[1,4096,6400]{2,1,0:T(8,128)(2,1)} %get-tuple-element.108, bf16[8,384,4096]{2,1,0:T(8,128)(2,1)} %get-tuple-element.107, s32[]{:T(128)} %get-tuple-element.98), kind=kOutput, calls=%fused_computation.4.clone.1 | convolution fusion | flops 20132659200 | bytes 65405440 | tf_op jit(solution)/shard_map/while/body/eval_jaxpr/dot_general | solution.py:30
  697.3 31.6 %fusion.9.clone.12 = bf16[384,6400]{1,0:T(8,128)(2,1)} fusion(bf16[1,4096,6400]{2,1,0:T(8,128)(2,1)} %get-tuple-element.109, f32[384,6400]{1,0:T(8,128)} %fusion.78, bf16[8,384,4096]{2,1,0:T(8,128)(2,1)} %get-tuple-element.107, s32[]{:T(128)} %get-tuple-element.98), kind=kOutput, calls=%fused_computation.7.clone.clone.clone.clone.clone.clone.clone.clone.clone.1.clone.1 | convolution fusion | flops 20147404800 | bytes 70320640 | tf_op jit(solution)/shard_map/while/body/eval_jaxpr/dot_general | solution.py:31
  728.9 28.0 %fusion.79 = bf16[8,384,4096]{2,1,0:T(8,128)(2,1)} fusion(bf16[8,384,4096]{2,1,0:T(8,128)(2,1)} %get-tuple-element.99, s32[]{:T(128)} %get-tuple-element.98, bf16[1,6400,4096]{2,1,0:T(8,128)(2,1)} %get-tuple-element.110, bf16[384,6400]{1,0:T(8,128)(2,1)} %fusion.9.clone.12), kind=kOutput, calls=%fused_computation.10.clone.2 | convolution fusion | flops 20134232064 | bytes 60490240 | tf_op jit(solution)/shard_map/while/body/eval_jaxpr/dot_general | solution.py:33
  757.0 31.1 %fusion.78 = f32[384,6400]{1,0:T(8,128)} fusion(bf16[1,4096,6400]{2,1,0:T(8,128)(2,1)} %get-tuple-element.108, bf16[8,384,4096]{2,1,0:T(8,128)(2,1)} %get-tuple-element.107, s32[]{:T(128)} %get-tuple-element.98), kind=kOutput, calls=%fused_computation.4.clone.1 | convolution fusion | flops 20132659200 | bytes 65405440 | tf_op jit(solution)/shard_map/while/body/eval_jaxpr/dot_general | solution.py:30
  788.1 31.6 %fusion.9.clone.12 = bf16[384,6400]{1,0:T(8,128)(2,1)} fusion(bf16[1,4096,6400]{2,1,0:T(8,128)(2,1)} %get-tuple-element.109, f32[384,6400]{1,0:T(8,128)} %fusion.78, bf16[8,384,4096]{2,1,0:T(8,128)(2,1)} %get-tuple-element.107, s32[]{:T(128)} %get-tuple-element.98), kind=kOutput, calls=%fused_computation.7.clone.clone.clone.clone.clone.clone.clone.clone.clone.1.clone.1 | convolution fusion | flops 20147404800 | bytes 70320640 | tf_op jit(solution)/shard_map/while/body/eval_jaxpr/dot_general | solution.py:31
  819.7 28.0 %fusion.79 = bf16[8,384,4096]{2,1,0:T(8,128)(2,1)} fusion(bf16[8,384,4096]{2,1,0:T(8,128)(2,1)} %get-tuple-element.99, s32[]{:T(128)} %get-tuple-element.98, bf16[1,6400,4096]{2,1,0:T(8,128)(2,1)} %get-tuple-element.110, bf16[384,6400]{1,0:T(8,128)(2,1)} %fusion.9.clone.12), kind=kOutput, calls=%fused_computation.10.clone.2 | convolution fusion | flops 20134232064 | bytes 60490240 | tf_op jit(solution)/shard_map/while/body/eval_jaxpr/dot_general | solution.py:33
  847.7 31.2 %fusion.78 = f32[384,6400]{1,0:T(8,128)} fusion(bf16[1,4096,6400]{2,1,0:T(8,128)(2,1)} %get-tuple-element.108, bf16[8,384,4096]{2,1,0:T(8,128)(2,1)} %get-tuple-element.107, s32[]{:T(128)} %get-tuple-element.98), kind=kOutput, calls=%fused_computation.4.clone.1 | convolution fusion | flops 20132659200 | bytes 65405440 | tf_op jit(solution)/shard_map/while/body/eval_jaxpr/dot_general | solution.py:30
  878.9 31.6 %fusion.9.clone.12 = bf16[384,6400]{1,0:T(8,128)(2,1)} fusion(bf16[1,4096,6400]{2,1,0:T(8,128)(2,1)} %get-tuple-element.109, f32[384,6400]{1,0:T(8,128)} %fusion.78, bf16[8,384,4096]{2,1,0:T(8,128)(2,1)} %get-tuple-element.107, s32[]{:T(128)} %get-tuple-element.98), kind=kOutput, calls=%fused_computation.7.clone.clone.clone.clone.clone.clone.clone.clone.clone.1.clone.1 | convolution fusion | flops 20147404800 | bytes 70320640 | tf_op jit(solution)/shard_map/while/body/eval_jaxpr/dot_general | solution.py:31
  910.5 28.0 %fusion.79 = bf16[8,384,4096]{2,1,0:T(8,128)(2,1)} fusion(bf16[8,384,4096]{2,1,0:T(8,128)(2,1)} %get-tuple-element.99, s32[]{:T(128)} %get-tuple-element.98, bf16[1,6400,4096]{2,1,0:T(8,128)(2,1)} %get-tuple-element.110, bf16[384,6400]{1,0:T(8,128)(2,1)} %fusion.9.clone.12), kind=kOutput, calls=%fused_computation.10.clone.2 | convolution fusion | flops 20134232064 | bytes 60490240 | tf_op jit(solution)/shard_map/while/body/eval_jaxpr/dot_general | solution.py:33
  938.6 31.1 %fusion.78 = f32[384,6400]{1,0:T(8,128)} fusion(bf16[1,4096,6400]{2,1,0:T(8,128)(2,1)} %get-tuple-element.108, bf16[8,384,4096]{2,1,0:T(8,128)(2,1)} %get-tuple-element.107, s32[]{:T(128)} %get-tuple-element.98), kind=kOutput, calls=%fused_computation.4.clone.1 | convolution fusion | flops 20132659200 | bytes 65405440 | tf_op jit(solution)/shard_map/while/body/eval_jaxpr/dot_general | solution.py:30
  969.7 31.7 %fusion.9.clone.12 = bf16[384,6400]{1,0:T(8,128)(2,1)} fusion(bf16[1,4096,6400]{2,1,0:T(8,128)(2,1)} %get-tuple-element.109, f32[384,6400]{1,0:T(8,128)} %fusion.78, bf16[8,384,4096]{2,1,0:T(8,128)(2,1)} %get-tuple-element.107, s32[]{:T(128)} %get-tuple-element.98), kind=kOutput, calls=%fused_computation.7.clone.clone.clone.clone.clone.clone.clone.clone.clone.1.clone.1 | convolution fusion | flops 20147404800 | bytes 70320640 | tf_op jit(solution)/shard_map/while/body/eval_jaxpr/dot_general | solution.py:31
  1001.4 28.0 %fusion.79 = bf16[8,384,4096]{2,1,0:T(8,128)(2,1)} fusion(bf16[8,384,4096]{2,1,0:T(8,128)(2,1)} %get-tuple-element.99, s32[]{:T(128)} %get-tuple-element.98, bf16[1,6400,4096]{2,1,0:T(8,128)(2,1)} %get-tuple-element.110, bf16[384,6400]{1,0:T(8,128)(2,1)} %fusion.9.clone.12), kind=kOutput, calls=%fused_computation.10.clone.2 | convolution fusion | flops 20134232064 | bytes 60490240 | tf_op jit(solution)/shard_map/while/body/eval_jaxpr/dot_general | solution.py:33
  1029.4 0.0 copy-start
  1029.4 0.0 copy-start.4
  1029.4 7.5 all-to-all-start.1
  1036.9 0.0 copy-done
  1036.9 273.4 %all-to-all-done.1 = bf16[8,384,4096]{2,1,0:T(8,128)(2,1)} async-done(((bf16[8,384,4096]{2,1,0:T(8,128)(2,1)}), bf16[8,384,4096]{2,1,0:T(8,128)(2,1)}, u32[]{:S(2)}, u32[]{:S(2)}) %all-to-all-start.1) | async-done | bytes 25165856 | tf_op jit(solution)/shard_map/all_to_all | solution.py:46
  1310.3 0.0 copy-done.4
  1310.3 0.0 copy-start.2
  1310.3 20.0 %fusion.40 = f32[512,4096]{1,0:T(8,128)} fusion(bf16[3072,4096]{1,0:T(8,128)(2,1)} %bitcast.9, s32[512]{0:T(512)S(1)} %bitcast.74), kind=kOutput, calls=%fused_computation.24 | convolution fusion | flops 12886474752 | bytes 33556480 | tf_op jit(solution)/shard_map/dot_general | solution.py:24
  1330.3 0.0 copy-done.2
  1330.3 20.6 %add_convert_fusion = bf16[512,4096]{1,0:T(8,128)(2,1)} fusion(f32[512,4096]{1,0:T(8,128)} %fusion.40, bf16[3072,4096]{1,0:T(8,128)(2,1)} %bitcast.9, f32[512]{0:T(512)S(1)} %bitcast.76, f32[512]{0:T(512)S(1)} %bitcast.75, s32[512]{0:T(512)S(1)} %bitcast.72), kind=kOutput, calls=%fused_computation.19 | convolution fusion | flops 12894863360 | bytes 37754880 | tf_op jit(solution)/shard_map/dot_general | solution.py:25
  (3 shorter events, 0.0 us)
Async XLA Ops:
  2.4 19.0 %copy-start.1 = (s32[512,1]{0,1:T(1,128)}, s32[512,1]{0,1:T(1,128)S(1)}, u32[]{:S(2)}) copy-start(s32[512,1]{0,1:T(1,128)S(1)} %get-tuple-element.53) | copy-start | bytes 6148
  2.4 19.0 %copy-start.3 = (s32[512,1]{0,1:T(1,128)}, s32[512,1]{0,1:T(1,128)S(1)}, u32[]{:S(2)}) copy-start(s32[512,1]{0,1:T(1,128)S(1)} %get-tuple-element.52) | copy-start | bytes 6148
  21.4 281.7 %all-to-all-start = ((bf16[8,384,4096]{2,1,0:T(8,128)(2,1)}), bf16[8,384,4096]{2,1,0:T(8,128)(2,1)}, u32[]{:S(2)}, u32[]{:S(2)}) async-start(bf16[8,384,4096]{2,1,0:T(8,128)(2,1)} %bitcast.70), calls=%async_computation | async-start | bytes 50331648 | tf_op jit(solution)/shard_map/all_to_all | solution.py:44
  1029.4 7.5 copy-start
  1029.4 280.9 %copy-start.4 = (s32[512,1]{0,1:T(1,128)S(1)}, s32[512,1]{0,1:T(1,128)}, u32[]{:S(2)}) copy-start(s32[512,1]{0,1:T(1,128)} %copy-done.3) | copy-start | bytes 6148
  1029.4 280.9 %all-to-all-start.1 = ((bf16[8,384,4096]{2,1,0:T(8,128)(2,1)}), bf16[8,384,4096]{2,1,0:T(8,128)(2,1)}, u32[]{:S(2)}, u32[]{:S(2)}) async-start(bf16[8,384,4096]{2,1,0:T(8,128)(2,1)} %get-tuple-element.37), calls=%async_computation.1 | async-start | bytes 50331648 | tf_op jit(solution)/shard_map/all_to_all | solution.py:46
  1310.3 20.0 %copy-start.2 = (s32[512,1]{0,1:T(1,128)S(1)}, s32[512,1]{0,1:T(1,128)}, u32[]{:S(2)}) copy-start(s32[512,1]{0,1:T(1,128)} %copy-done.1) | copy-start | bytes 6148
where the time goes:
time: 1350 us
  matrix products  786 us (58%)
  waiting for transfers between devices  547 us (41%)
  starting transfers between devices  15.8 us (1%)
    all_to_all x1, waiting for transfers between devices, local(): recv = lax.all_to_all(send, 'ep', 0, 0, tiled=True)  273 us
    all_to_all x1, waiting for transfers between devices, local(): back = lax.all_to_all(out, 'ep', 0, 0, tiled=True)  273 us
    dot_general x8, matrix products, expert_rows(): b = jnp.dot(rows, w3, preferred_element_type=jnp.float32)  253 us
    dot_general x8, matrix products, expert_rows(): a = jnp.dot(rows, w1, preferred_element_type=jnp.float32)  249 us
    dot_general x8, matrix products, expert_rows(): jnp.dot(h, w2, preferred_element_type=jnp.float32).astype(jnp.bfloat16)  224 us
  transfers between devices with their start and end apart: 2, of which 2 were waited for; matrix products, arithmetic and copies ran while one was open for 0% of the time, Pallas kernels for 0%

commit v1 on v0

v1 whole, which is shorter than its diff:
```python
import functools

import jax
import jax.numpy as jnp
from jax import lax
from jax.experimental import pallas as pl
from jax.experimental.pallas import tpu as pltpu
from jax.sharding import PartitionSpec as P

CHUNKS = (96, 128, 144, 144)
TN = 256
WIN = 256
SIZES = (4, 8, 9, 10)
TD = 256


def row_tiles(n, rows, body):
    sizes = [(rows * k + 255) // 256 * 16 for k in SIZES]
    step = rows // 2
    nbig = jnp.maximum(n - sizes[-1] + step - 1, 0) // step

    def big(i, _):
        body(pl.multiple_of(i * step, 16), step)
        return 0

    lax.fori_loop(0, nbig, big, 0)
    off = pl.multiple_of(nbig * step, 16)
    rest = n - off
    low = 0
    for size in sizes:
        pl.when((rest > low) & (rest <= size))(functools.partial(body, off, size))
        low = size


def ffn_kernel(base_ref, dl_ref, dc_ref, x_hbm, w1_hbm, w3_hbm, w2_hbm, o_hbm,
               xg, xc, h, up, down, oc, sel, obuf, x_sem, up_sem, down_sem, o_sem):
    nb, tok = dl_ref.shape
    d = xg.shape[1]
    ff = h.shape[1]
    nup = ff // TN
    ndown = d // TD
    n = base_ref[nb]

    def up_copies(i):
        slot = lax.rem(i, 2)
        cols = pl.ds(pl.multiple_of(i * TN, TN), TN)
        return [pltpu.make_async_copy(src.at[:, cols], up.at[slot, k], up_sem.at[slot, k])
                for k, src in enumerate((w1_hbm, w3_hbm))]

    def down_copies(i):
        slot = lax.rem(i, 2)
        cols = pl.ds(pl.multiple_of(i * TD, TD), TD)
        return [pltpu.make_async_copy(w2_hbm.at[:, cols], down.at[slot], down_sem.at[slot])]

    def start(copies):
        for copy in copies:
            copy.start()

    def wait(copies):
        for copy in copies:
            copy.wait()

    def out_copy(i):
        slot = lax.rem(i, 2)
        return pltpu.make_async_copy(obuf.at[slot], o_hbm.at[:, pl.ds(pl.multiple_of(i * TD, TD), TD)],
                                     o_sem.at[slot])

    x_copy = pltpu.make_async_copy(x_hbm, xg, x_sem)
    x_copy.start()
    start(up_copies(0))
    start(down_copies(0))
    oc[...] = jnp.zeros_like(oc)
    for b in range(nb):
        al = (base_ref[b] // 16) * 16
        k = lax.broadcasted_iota(jnp.int32, (tok, WIN), 1)
        sel[pl.ds(b * tok, tok), :] = jnp.where(dc_ref[pl.ds(b * tok, tok), :] - al == k, 1.0, 0.0).astype(sel.dtype)
    x_copy.wait()

    for b in range(nb):
        base = base_ref[b]
        al = pl.multiple_of((base // 16) * 16, 16)
        r = lax.broadcasted_iota(jnp.int32, (WIN, tok), 0)
        p = jnp.where(dl_ref[b:b + 1, :] - al == r, 1.0, 0.0).astype(xg.dtype)
        new = jnp.dot(p, xg[pl.ds(b * tok, tok), :], preferred_element_type=jnp.float32).astype(xc.dtype)
        if b == 0:
            xc[pl.ds(0, WIN), :] = new
        else:
            keep = lax.broadcasted_iota(jnp.int32, (16, d), 0) < base - al
            old = xc[pl.ds(al, 16), :].astype(jnp.float32)
            head = jnp.where(keep, old, new[:16].astype(jnp.float32)).astype(xc.dtype)
            xc[pl.ds(al, 16), :] = head
            xc[pl.ds(al + 16, WIN - 16), :] = new[16:]

    def up_step(i, _):
        slot = lax.rem(i, 2)
        wait(up_copies(i))

        @pl.when(i + 1 < nup)
        def _():
            start(up_copies(i + 1))

        def body(off, size):
            rows = xc[pl.ds(off, size), :]
            a = jnp.dot(rows, up[slot, 0], preferred_element_type=jnp.float32)
            b = jnp.dot(rows, up[slot, 1], preferred_element_type=jnp.float32)
            h[pl.ds(off, size), pl.ds(pl.multiple_of(i * TN, TN), TN)] = (jax.nn.silu(a) * b).astype(h.dtype)

        row_tiles(n, h.shape[0], body)
        return 0

    lax.fori_loop(0, nup, up_step, 0)

    def down_step(i, _):
        slot = lax.rem(i, 2)
        wait(down_copies(i))

        @pl.when(i + 1 < ndown)
        def _():
            start(down_copies(i + 1))

        @pl.when(i >= 2)
        def _():
            out_copy(i - 2).wait()

        def body(off, size):
            oc[pl.ds(off, size), :] = jnp.dot(h[pl.ds(off, size), :], down[slot],
                                              preferred_element_type=jnp.float32).astype(oc.dtype)

        row_tiles(n, h.shape[0], body)
        for b in range(nb):
            al = pl.multiple_of((base_ref[b] // 16) * 16, 16)
            obuf[slot, pl.ds(b * tok, tok), :] = jnp.dot(
                sel[pl.ds(b * tok, tok), :], oc[pl.ds(al, WIN), :],
                preferred_element_type=jnp.float32).astype(obuf.dtype)
        out_copy(i).start()
        return 0

    lax.fori_loop(0, ndown, down_step, 0)
    out_copy(ndown - 2).wait()
    out_copy(ndown - 1).wait()


def expert_rows(base, dl, x, w1, w3, w2):
    nb, tok = dl.shape
    rows, d = x.shape
    ff = w1.shape[1]
    bf = jnp.bfloat16
    smem = pl.BlockSpec(memory_space=pltpu.SMEM)
    vmem = pl.BlockSpec(memory_space=pltpu.VMEM)
    hbm = pl.BlockSpec(memory_space=pl.ANY)
    return pl.pallas_call(
        ffn_kernel,
        out_shape=jax.ShapeDtypeStruct((rows, d), x.dtype),
        in_specs=[smem, vmem, vmem, hbm, hbm, hbm, hbm],
        out_specs=hbm,
        scratch_shapes=[
            pltpu.VMEM((rows, d), bf),
            pltpu.VMEM((rows + WIN, d), bf),
            pltpu.VMEM((rows, ff), bf),
            pltpu.VMEM((2, 2, d, TN), bf),
            pltpu.VMEM((2, ff, TD), bf),
            pltpu.VMEM((rows + WIN, TD), bf),
            pltpu.VMEM((rows, WIN), bf),
            pltpu.VMEM((2, rows, TD), bf),
            pltpu.SemaphoreType.DMA,
            pltpu.SemaphoreType.DMA((2, 2)),
            pltpu.SemaphoreType.DMA((2,)),
            pltpu.SemaphoreType.DMA((2,)),
        ],
        compiler_params=pltpu.CompilerParams(vmem_limit_bytes=66000000),
        cost_estimate=pl.CostEstimate(flops=rows * d * ff * 3, transcendentals=rows * ff,
                                      bytes_accessed=3 * d * ff * 2 + 4 * rows * d),
        name='ffn',
    )(base, dl, dl.reshape(rows, 1), x, w1, w3, w2)


def solution(mesh):
    ep = mesh.shape['ep']

    def local(x, route_idx, gates, w1, w3, w2):
        tok, d = x.shape
        me = lax.axis_index('ep')
        ids = lax.all_gather(route_idx, 'ep')
        hit = jnp.any(ids == me, axis=2)
        table = jnp.sum(jnp.where(route_idx[:, :, None] == jnp.arange(ep, dtype=route_idx.dtype),
                                  gates[:, :, None], 0.0), axis=1)
        t = jnp.arange(tok)
        first = jnp.zeros((tok,), jnp.int32)
        starts = []
        for size in CHUNKS:
            starts.append(sum(CHUNKS[:len(starts)]))
            first = jnp.where(t >= starts[-1], starts[-1], first)
        low = ((t[:, None] < t[None, :]) & (t[:, None] >= first[None, :])).astype(jnp.bfloat16)
        before = jnp.dot(hit.astype(jnp.bfloat16), low, preferred_element_type=jnp.float32).astype(jnp.int32)
        hits = hit.astype(jnp.int32)
        ys = []
        for s, size in zip(starts, CHUNKS):
            part = slice(s, s + size)
            total = jnp.cumsum(jnp.sum(hits[:, part], axis=1))
            base = jnp.concatenate([jnp.zeros((1,), jnp.int32), total])
            dest = jnp.where(hit[:, part], before[:, part] + base[:ep, None], -1)
            xs = lax.all_gather(x[part], 'ep').reshape(ep * size, d)
            o = expert_rows(base, dest, xs, w1[0], w3[0], w2[0])
            back = lax.all_to_all(o.reshape(ep, size, d), 'ep', 0, 0, tiled=True)
            g = table[part]
            y = g[:, 0:1] * back[0].astype(jnp.float32)
            for j in range(1, ep):
                y = y + g[:, j:j + 1] * back[j].astype(jnp.float32)
            ys.append(y.astype(x.dtype))
        return jnp.concatenate(ys, axis=0)

    spec = P(('dp', 'ep'), None)
    wspec = P('ep', None, None)
    return jax.shard_map(local, mesh=mesh, in_specs=(spec, spec, spec, wspec, wspec, wspec),
                         out_specs=spec, check_vma=False)
```

time: 1350 us -> 643 us (0.48)
  matrix products: 786 us -> 0.26 us
  Pallas kernels: 0 us -> 438 us
  waiting for transfers between devices: 547 us -> 110 us
  other arithmetic: 2.13 us -> 21.9 us
  blocking collectives: 0 us -> 14.9 us
  between operations: 0.03 us -> 13.9 us
    dot_general x28 -> x1, matrix products: 786 us -> 0.26 us  [local(): jnp.dot(hit.astype(jnp.bfloat16), low, preferred_element_type=jnp.float32)]
    all_to_all x2 -> x4, waiting for transfers between devices: 547 us -> 94.4 us  [local(): back = lax.all_to_all(o.reshape(ep, size, d), 'ep', 0, 0, tiled=True)]
    pallas_call x0 -> x4, Pallas kernels: none -> 438 us  [expert_rows(): pl.pallas_call(ffn_kernel, out_shape=jax.ShapeDtypeStruct((rows, d), x.dt...]
    convert_element_type x0 -> x5, other arithmetic: none -> 17.9 us  [the longest x4 17.9 us: local(): ys.append(y.astype(x.dtype))]
    all_gather x0 -> x1, blocking collectives: none -> 14.9 us  [local(): ids = lax.all_gather(route_idx, 'ep')]
    all_gather x0 -> x4, waiting for transfers between devices: none -> 14.6 us  [local(): xs = lax.all_gather(x[part], 'ep').reshape(ep * size, d)]
  transfers between devices with their start and end apart: 2 -> 8, of which waited for: 2 -> 3; matrix products, arithmetic and copies ran while one was open for 0% -> 4% of each run, Pallas kernels for 0% -> 69%
where the time goes in v1:
time: 643 us; the launch traced here: 634 us
  Pallas kernels  438 us (68%)
  waiting for transfers between devices  110 us (17%)
  starting transfers between devices  22.3 us (3%)
  other arithmetic  21.9 us (3%)
  blocking collectives  14.9 us (2%)
  between operations  13.9 us (2%)
  local copies, waits for them, and re-layouts  12.4 us (2%)
    pallas_call x4, Pallas kernels, expert_rows(): pl.pallas_call(ffn_kernel, out_shape=jax.ShapeDtypeStruct((rows, d), x.dt...  438 us
    all_to_all x4, waiting for transfers between devices, local(): back = lax.all_to_all(o.reshape(ep, size, d), 'ep', 0, 0, tiled=True)  94.4 us
    all_to_all x4, starting transfers between devices, local(): back = lax.all_to_all(o.reshape(ep, size, d), 'ep', 0, 0, tiled=True)  22.1 us
    convert_element_type x4, other arithmetic, local(): ys.append(y.astype(x.dtype))  17.9 us
    all_gather x1, blocking collectives, local(): ids = lax.all_gather(route_idx, 'ep')  14.9 us
    all_gather x4, waiting for transfers between devices, local(): xs = lax.all_gather(x[part], 'ep').reshape(ep * size, d)  14.6 us
  transfers between devices with their start and end apart: 8, of which 3 were waited for; matrix products, arithmetic and copies ran while one was open for 4% of the time, Pallas kernels for 69%

profile of v1, /device:TPU:81, one launch (start us, length us, event | category | flops | bytes accessed | tf_op | source)
XLA Modules:
  0.0 633.8 jit_solution(15403885116471879574)
XLA Ops:
  6.6 2.1 slice.293
  8.6 0.1 all-gather.10.cloned.1.call-update
  8.7 0.1 all-gather.12.cloned.1.call-start
  8.8 2.3 slice.314
  11.1 0.1 all-gather.14.cloned.1.call-start
  11.2 3.3 fusion.39
  14.5 0.1 all-gather.16.cloned.1.call-start
  14.6 0.6 all-gather.16.cloned.1.call-update
  15.2 14.9 %all-gather = s32[4096,2]{0,1:T(2,128)S(1)} all-gather(s32[512,2]{0,1:T(2,128)S(1)} %copy-done.4), channel_id=2, replica_groups=mesh['dp'=4,'ep'=8] {'ep'}, dimensions={0}, use_global_device_ids=true | all-gather | bytes 36864 | tf_op jit(solution)/shard_map/all_gather | solution.py:183
  30.1 0.1 compare_reduce_fusion
  30.2 0.2 slice_reduce_fusion.1
  30.3 0.2 slice_reduce_fusion.2
  30.5 0.1 slice_reduce_fusion.3
  30.6 0.2 reduce-window.38
  30.8 0.2 reduce-window.39
  31.0 0.1 pad_add_fusion.1.base_ref
  31.1 0.1 pad_add_fusion.base_ref
  31.2 0.3 convolution_convert_fusion
  31.4 0.3 copy-done.7
  31.7 0.1 fusion.36
  31.8 1.1 reshape.286.dc_ref
  32.9 1.1 reshape.287.dc_ref
  34.0 0.2 reduce-window.37
  34.2 0.1 pad_add_fusion.2.base_ref
  34.3 0.1 fusion.37.dl_ref
  34.3 1.0 copy.19.dc_ref
  35.4 0.2 reduce-window.36
  35.6 0.1 pad_add_fusion.3.base_ref
  35.6 0.1 fusion.38.dl_ref
  35.7 1.0 reshape.285.dc_ref
  36.7 14.5 %all-gather.10.cloned.1.call-done.x_hbm = bf16[768,4096]{1,0:T(8,128)(2,1)} async-done(((bf16[96,4096]{1,0:T(8,128)(2,1)}), bf16[768,4096]{1,0:T(8,128)(2,1)}) %all-gather.10.cloned.1.call-update) | async-done | bytes 6291472 | tf_op jit(solution)/shard_map/all_gather | solution.py:202
  51.2 97.9 %ffn.4 = bf16[768,4096]{1,0:T(8,128)(2,1)} custom-call(s32[9]{0:T(128)} %copy-done.10, s32[8,96]{1,0:T(8,128)} %copy-done.3, s32[768,1]{1,0:T(8,128)} %reshape.285.dc_ref, bf16[768,4096]{1,0:T(8,128)(2,1)} %all-gather.10.cloned.1.call-done.x_hbm, bf16[4096,6400]{1,0:T(8,128)(2,1)} %bitcast.258, bf16[4096,6400]{1,0:T(8,128)(2,1)} %bitcast.262, ...), custom_call_target="tpu_custom_call" | custom-call | flops 60397977600 | bytes 169869312 | tf_op jit(solution)/shard_map/ffn/pallas_call | solution.py:151
  149.2 5.2 all-to-all-start
  154.4 106.0 %ffn.5 = bf16[1024,4096]{1,0:T(8,128)(2,1)} custom-call(s32[9]{0:T(128)} %copy-done.9, s32[8,128]{1,0:T(8,128)} %copy-done.2, s32[1024,1]{1,0:T(8,128)} %copy.19.dc_ref, bf16[1024,4096]{1,0:T(8,128)(2,1)} %all-gather.12.cloned.1.call-done.x_hbm, bf16[4096,6400]{1,0:T(8,128)(2,1)} %bitcast.259, bf16[4096,6400]{1,0:T(8,128)(2,1)} %bitcast.263, ...), custom_call_target="tpu_custom_call" | custom-call | flops 80530636800 | bytes 174063616 | tf_op jit(solution)/shard_map/ffn/pallas_call | solution.py:151
  260.4 2.9 all-to-all-done
  263.3 6.3 all-to-all-start.1
  269.7 117.3 %ffn.6 = bf16[1152,4096]{1,0:T(8,128)(2,1)} custom-call(s32[9]{0:T(128)} %copy-done.8, s32[8,144]{1,0:T(8,128)} %copy-done.1, s32[1152,1]{1,0:T(8,128)} %reshape.286.dc_ref, bf16[1152,4096]{1,0:T(8,128)(2,1)} %all-gather.14.cloned.1.call-done.x_hbm, bf16[4096,6400]{1,0:T(8,128)(2,1)} %bitcast.260, bf16[4096,6400]{1,0:T(8,128)(2,1)} %bitcast.264, ...), custom_call_target="tpu_custom_call" | custom-call | flops 90596966400 | bytes 176160768 | tf_op jit(solution)/shard_map/ffn/pallas_call | solution.py:151
  387.0 5.4 all-to-all-start.2
  392.5 117.3 %ffn.7 = bf16[1152,4096]{1,0:T(8,128)(2,1)} custom-call(s32[9]{0:T(128)} %copy-done.7, s32[8,144]{1,0:T(8,128)} %copy-done, s32[1152,1]{1,0:T(8,128)} %reshape.287.dc_ref, bf16[1152,4096]{1,0:T(8,128)(2,1)} %all-gather.16.cloned.1.call-done.x_hbm, bf16[4096,6400]{1,0:T(8,128)(2,1)} %bitcast.261, bf16[4096,6400]{1,0:T(8,128)(2,1)} %bitcast.265, ...), custom_call_target="tpu_custom_call" | custom-call | flops 90596966400 | bytes 176160768 | tf_op jit(solution)/shard_map/ffn/pallas_call | solution.py:151
  509.8 5.1 all-to-all-start.3
  515.0 0.1 slice_bitcast_fusion.39
  515.0 0.1 fusion.40
  515.1 3.6 fusion.25
  518.8 4.5 fusion.17
  523.3 4.9 fusion.9
  528.2 91.5 %all-to-all-done.3 = bf16[8,144,4096]{2,1,0:T(8,128)(2,1)} async-done(((bf16[8,144,4096]{2,1,0:T(8,128)(2,1)}), bf16[8,144,4096]{2,1,0:T(8,128)(2,1)}, u32[]{:S(2)}, u32[]{:S(2)}) %all-to-all-start.3) | async-done | bytes 9437216 | tf_op jit(solution)/shard_map/all_to_all | solution.py:204
  619.7 4.9 fusion.1
  624.6 2.2 pad_maximum_fusion
  (34 shorter events, 0.3 us)
Async XLA Ops:
  6.5 44.7 %all-gather.10.cloned.1.call-start = ((), (), s32[]{:S(2)}) async-start(), calls=%async_computation.4 | async-start | bytes 7077888 | tf_op jit(solution)/shard_map/all_gather | solution.py:202
  8.7 145.7 %all-gather.12.cloned.1.call-start = ((), (), s32[]{:S(2)}) async-start(), calls=%async_computation.5 | async-start | bytes 9437184 | tf_op jit(solution)/shard_map/all_gather | solution.py:202
  11.1 258.5 %all-gather.14.cloned.1.call-start = ((), (), s32[]{:S(2)}) async-start(), calls=%async_computation.6 | async-start | bytes 10616832 | tf_op jit(solution)/shard_map/all_gather | solution.py:202
  14.5 0.7 copy-start.4
  14.5 377.9 %all-gather.16.cloned.1.call-start = ((), (), s32[]{:S(2)}) async-start(), calls=%async_computation.7 | async-start | bytes 10616832 | tf_op jit(solution)/shard_map/all_gather | solution.py:202
  31.1 0.7 copy-start.8
  31.2 0.6 copy-start.7
  31.8 3.9 copy-start
  31.8 4.9 copy-start.1
  34.3 114.9 %copy-start.9 = (s32[9]{0:T(128)}, s32[9]{0:T(128)S(1)}, u32[]{:S(2)}) copy-start(s32[9]{0:T(128)S(1)} %pad_add_fusion.2.base_ref) | copy-start | bytes 112
  34.3 114.8 %copy-start.2 = (s32[8,128]{1,0:T(8,128)}, s32[8,128]{1,0:T(8,128)S(1)}, u32[]{:S(2)}) copy-start(s32[8,128]{1,0:T(8,128)S(1)} %fusion.37.dl_ref) | copy-start | bytes 12292
  35.6 15.6 %copy-start.10 = (s32[9]{0:T(128)}, s32[9]{0:T(128)S(1)}, u32[]{:S(2)}) copy-start(s32[9]{0:T(128)S(1)} %pad_add_fusion.3.base_ref) | copy-start | bytes 112
  35.7 15.5 %copy-start.3 = (s32[8,96]{1,0:T(8,128)}, s32[8,96]{1,0:T(8,128)S(1)}, u32[]{:S(2)}) copy-start(s32[8,96]{1,0:T(8,128)S(1)} %fusion.38.dl_ref) | copy-start | bytes 9220
  149.2 114.2 %all-to-all-start = ((bf16[8,96,4096]{2,1,0:T(8,128)(2,1)}), bf16[8,96,4096]{2,1,0:T(8,128)(2,1)}, u32[]{:S(2)}, u32[]{:S(2)}) async-start(bf16[8,96,4096]{2,1,0:T(8,128)(2,1)} %bitcast.232), calls=%async_computation | async-start | bytes 12582912 | tf_op jit(solution)/shard_map/all_to_all | solution.py:204
  263.3 123.7 %all-to-all-start.1 = ((bf16[8,128,4096]{2,1,0:T(8,128)(2,1)}), bf16[8,128,4096]{2,1,0:T(8,128)(2,1)}, u32[]{:S(2)}, u32[]{:S(2)}) async-start(bf16[8,128,4096]{2,1,0:T(8,128)(2,1)} %bitcast.231), calls=%async_computation.1 | async-start | bytes 16777216 | tf_op jit(solution)/shard_map/all_to_all | solution.py:204
  387.0 122.8 %all-to-all-start.2 = ((bf16[8,144,4096]{2,1,0:T(8,128)(2,1)}), bf16[8,144,4096]{2,1,0:T(8,128)(2,1)}, u32[]{:S(2)}, u32[]{:S(2)}) async-start(bf16[8,144,4096]{2,1,0:T(8,128)(2,1)} %bitcast.230), calls=%async_computation.2 | async-start | bytes 18874368 | tf_op jit(solution)/shard_map/all_to_all | solution.py:204
  509.8 5.2 copy-start.5
  509.8 5.2 copy-start.6
  509.8 109.9 %all-to-all-start.3 = ((bf16[8,144,4096]{2,1,0:T(8,128)(2,1)}), bf16[8,144,4096]{2,1,0:T(8,128)(2,1)}, u32[]{:S(2)}, u32[]{:S(2)}) async-start(bf16[8,144,4096]{2,1,0:T(8,128)(2,1)} %bitcast.229), calls=%async_computation.3 | async-start | bytes 18874368 | tf_op jit(solution)/shard_map/all_to_all | solution.py:204
Sparse Core Ops, SparseCore 0:
  8.9 42.2 all-gather.9
  52.9 46.5 all-gather.11
  101.0 51.0 all-gather.13
  153.6 93.7 all-gather.15

commit v2 on v1

--- a/solution.py
+++ b/solution.py
@@ -7,7 +7,8 @@
 from jax.experimental.pallas import tpu as pltpu
 from jax.sharding import PartitionSpec as P
 
-CHUNKS = (96, 128, 144, 144)
+
+CHUNKS = (144, 144, 128, 96)
 TN = 256
 WIN = 256
 SIZES = (4, 8, 9, 10)
@@ -15,7 +16,7 @@
 
 
 def row_tiles(n, rows, body):
-    sizes = [(rows * k + 255) // 256 * 16 for k in SIZES]
+    sizes = [rows * k // 256 * 16 for k in SIZES]
     step = rows // 2
     nbig = jnp.maximum(n - sizes[-1] + step - 1, 0) // step
 
@@ -65,8 +66,9 @@
         return pltpu.make_async_copy(obuf.at[slot], o_hbm.at[:, pl.ds(pl.multiple_of(i * TD, TD), TD)],
                                      o_sem.at[slot])
 
-    x_copy = pltpu.make_async_copy(x_hbm, xg, x_sem)
-    x_copy.start()
+    x_copies = [pltpu.make_async_copy(x_hbm.at[pl.ds(b * tok, tok)], xg.at[pl.ds(b * tok, tok)], x_sem.at[b])
+                for b in range(nb)]
+    start(x_copies)
     start(up_copies(0))
     start(down_copies(0))
     oc[...] = jnp.zeros_like(oc)
@@ -74,9 +76,9 @@
         al = (base_ref[b] // 16) * 16
         k = lax.broadcasted_iota(jnp.int32, (tok, WIN), 1)
         sel[pl.ds(b * tok, tok), :] = jnp.where(dc_ref[pl.ds(b * tok, tok), :] - al == k, 1.0, 0.0).astype(sel.dtype)
-    x_copy.wait()
 
     for b in range(nb):
+        x_copies[b].wait()
         base = base_ref[b]
         al = pl.multiple_of((base // 16) * 16, 16)
         r = lax.broadcasted_iota(jnp.int32, (WIN, tok), 0)
@@ -141,7 +143,7 @@
 
 
 def expert_rows(base, dl, x, w1, w3, w2):
-    nb, tok = dl.shape
+    nb, _ = dl.shape
     rows, d = x.shape
     ff = w1.shape[1]
     bf = jnp.bfloat16
@@ -162,7 +164,7 @@
             pltpu.VMEM((rows + WIN, TD), bf),
             pltpu.VMEM((rows, WIN), bf),
             pltpu.VMEM((2, rows, TD), bf),
-            pltpu.SemaphoreType.DMA,
+            pltpu.SemaphoreType.DMA((nb,)),
             pltpu.SemaphoreType.DMA((2, 2)),
             pltpu.SemaphoreType.DMA((2,)),
             pltpu.SemaphoreType.DMA((2,)),
@@ -193,16 +195,18 @@
         low = ((t[:, None] < t[None, :]) & (t[:, None] >= first[None, :])).astype(jnp.bfloat16)
         before = jnp.dot(hit.astype(jnp.bfloat16), low, preferred_element_type=jnp.float32).astype(jnp.int32)
         hits = hit.astype(jnp.int32)
-        ys = []
+        outs = []
         for s, size in zip(starts, CHUNKS):
             part = slice(s, s + size)
             total = jnp.cumsum(jnp.sum(hits[:, part], axis=1))
             base = jnp.concatenate([jnp.zeros((1,), jnp.int32), total])
             dest = jnp.where(hit[:, part], before[:, part] + base[:ep, None], -1)
             xs = lax.all_gather(x[part], 'ep').reshape(ep * size, d)
-            o = expert_rows(base, dest, xs, w1[0], w3[0], w2[0])
+            outs.append(expert_rows(base, dest, xs, w1[0], w3[0], w2[0]))
+        ys = []
+        for s, size, o in zip(starts, CHUNKS, outs):
             back = lax.all_to_all(o.reshape(ep, size, d), 'ep', 0, 0, tiled=True)
-            g = table[part]
+            g = table[s:s + size]
             y = g[:, 0:1] * back[0].astype(jnp.float32)
             for j in range(1, ep):
                 y = y + g[:, j:j + 1] * back[j].astype(jnp.float32)

time: 643 us -> 642 us (level)
  no operation moved by 1% of the time
where the time goes in v2:
time: 642 us; the launch traced here: 632 us
  Pallas kernels  435 us (68%)
  waiting for transfers between devices  110 us (17%)
  starting transfers between devices  23.3 us (4%)
  other arithmetic  22 us (3%)
  blocking collectives  15.1 us (2%)
  between operations  13.6 us (2%)
  local copies, waits for them, and re-layouts  12.4 us (2%)
    pallas_call x4, Pallas kernels, expert_rows(): pl.pallas_call(ffn_kernel, out_shape=jax.ShapeDtypeStruct((rows, d), x.dt...  435 us
    all_to_all x4, waiting for transfers between devices, local(): back = lax.all_to_all(o.reshape(ep, size, d), 'ep', 0, 0, tiled=True)  95.2 us
    all_to_all x4, starting transfers between devices, local(): back = lax.all_to_all(o.reshape(ep, size, d), 'ep', 0, 0, tiled=True)  23.1 us
    convert_element_type x4, other arithmetic, local(): ys.append(y.astype(x.dtype))  17.9 us
    all_gather x1, blocking collectives, local(): ids = lax.all_gather(route_idx, 'ep')  15.1 us
    all_gather x4, waiting for transfers between devices, local(): xs = lax.all_gather(x[part], 'ep').reshape(ep * size, d)  14.5 us
  transfers between devices with their start and end apart: 8, of which 3 were waited for; matrix products, arithmetic and copies ran while one was open for 4% of the time, Pallas kernels for 69%

profile of v2, /device:TPU:81, one launch (start us, length us, event | category | flops | bytes accessed | tf_op | source)
XLA Modules:
  0.0 631.8 jit_solution(8734413785564393951)
XLA Ops:
  6.6 2.1 slice.356
  8.7 0.1 all-gather.14.cloned.1.call-start
  8.8 2.3 slice.335
  11.1 0.1 all-gather.12.cloned.1.call-start
  11.2 3.3 fusion.39
  14.5 0.1 all-gather.10.cloned.1.call-start
  14.6 0.6 all-gather.10.cloned.1.call-update
  15.2 15.1 %all-gather = s32[4096,2]{0,1:T(2,128)S(1)} all-gather(s32[512,2]{0,1:T(2,128)S(1)} %copy-done.4), channel_id=2, replica_groups=mesh['dp'=4,'ep'=8] {'ep'}, dimensions={0}, use_global_device_ids=true | all-gather | bytes 36864 | tf_op jit(solution)/shard_map/all_gather | solution.py:185
  30.2 0.1 compare_reduce_fusion
  30.3 0.2 slice_reduce_fusion.1
  30.5 0.2 slice_reduce_fusion.3
  30.7 0.2 slice_reduce_fusion.2
  30.9 0.2 reduce-window.36
  31.1 0.2 reduce-window.37
  31.3 0.1 pad_add_fusion.3.base_ref
  31.3 0.1 pad_add_fusion.2.base_ref
  31.4 0.3 convolution_convert_fusion
  31.7 0.2 copy-done.7
  31.9 0.1 fusion.36
  32.0 1.1 reshape.286.dc_ref
  33.1 1.1 reshape.285.dc_ref
  34.2 0.2 reduce-window.38
  34.3 0.1 pad_add_fusion.1.base_ref
  34.4 0.1 fusion.38.dl_ref
  34.5 1.0 copy.20.dc_ref
  35.5 0.2 reduce-window.39
  35.7 0.1 pad_add_fusion.base_ref
  35.8 0.1 fusion.37.dl_ref
  35.9 1.0 reshape.287.dc_ref
  36.9 14.5 %all-gather.16.cloned.1.call-done.x_hbm = bf16[768,4096]{1,0:T(8,128)(2,1)} async-done(((bf16[96,4096]{1,0:T(8,128)(2,1)}), bf16[768,4096]{1,0:T(8,128)(2,1)}) %all-gather.16.cloned.1.call-update) | async-done | bytes 6291472 | tf_op jit(solution)/shard_map/all_gather | solution.py:204
  51.4 98.4 %ffn.7 = bf16[768,4096]{1,0:T(8,128)(2,1)} custom-call(s32[9]{0:T(128)} %copy-done.10, s32[8,96]{1,0:T(8,128)} %copy-done.3, s32[768,1]{1,0:T(8,128)} %reshape.287.dc_ref, bf16[768,4096]{1,0:T(8,128)(2,1)} %all-gather.16.cloned.1.call-done.x_hbm, bf16[4096,6400]{1,0:T(8,128)(2,1)} %bitcast.258, bf16[4096,6400]{1,0:T(8,128)(2,1)} %bitcast.262, ...), custom_call_target="tpu_custom_call" | custom-call | flops 60397977600 | bytes 169869312 | tf_op jit(solution)/shard_map/ffn/pallas_call | solution.py:153
  149.8 6.5 %all-to-all-start.3 = ((bf16[8,96,4096]{2,1,0:T(8,128)(2,1)}), bf16[8,96,4096]{2,1,0:T(8,128)(2,1)}, u32[]{:S(2)}, u32[]{:S(2)}) async-start(bf16[8,96,4096]{2,1,0:T(8,128)(2,1)} %bitcast.232), calls=%async_computation.3 | async-start | bytes 12582912 | tf_op jit(solution)/shard_map/all_to_all | solution.py:208
  156.3 105.1 %ffn.6 = bf16[1024,4096]{1,0:T(8,128)(2,1)} custom-call(s32[9]{0:T(128)} %copy-done.9, s32[8,128]{1,0:T(8,128)} %copy-done.2, s32[1024,1]{1,0:T(8,128)} %copy.20.dc_ref, bf16[1024,4096]{1,0:T(8,128)(2,1)} %all-gather.14.cloned.1.call-done.x_hbm, bf16[4096,6400]{1,0:T(8,128)(2,1)} %bitcast.259, bf16[4096,6400]{1,0:T(8,128)(2,1)} %bitcast.263, ...), custom_call_target="tpu_custom_call" | custom-call | flops 80530636800 | bytes 174063616 | tf_op jit(solution)/shard_map/ffn/pallas_call | solution.py:153
  261.4 4.0 all-to-all-done.3
  265.4 6.1 all-to-all-start.2
  271.6 115.5 %ffn.5 = bf16[1152,4096]{1,0:T(8,128)(2,1)} custom-call(s32[9]{0:T(128)} %copy-done.8, s32[8,144]{1,0:T(8,128)} %copy-done.1, s32[1152,1]{1,0:T(8,128)} %reshape.286.dc_ref, bf16[1152,4096]{1,0:T(8,128)(2,1)} %all-gather.12.cloned.1.call-done.x_hbm, bf16[4096,6400]{1,0:T(8,128)(2,1)} %bitcast.260, bf16[4096,6400]{1,0:T(8,128)(2,1)} %bitcast.264, ...), custom_call_target="tpu_custom_call" | custom-call | flops 90596966400 | bytes 176160768 | tf_op jit(solution)/shard_map/ffn/pallas_call | solution.py:153
  387.1 5.4 all-to-all-start.1
  392.6 115.8 %ffn.4 = bf16[1152,4096]{1,0:T(8,128)(2,1)} custom-call(s32[9]{0:T(128)} %copy-done.7, s32[8,144]{1,0:T(8,128)} %copy-done, s32[1152,1]{1,0:T(8,128)} %reshape.285.dc_ref, bf16[1152,4096]{1,0:T(8,128)(2,1)} %all-gather.10.cloned.1.call-done.x_hbm, bf16[4096,6400]{1,0:T(8,128)(2,1)} %bitcast.261, bf16[4096,6400]{1,0:T(8,128)(2,1)} %bitcast.265, ...), custom_call_target="tpu_custom_call" | custom-call | flops 90596966400 | bytes 176160768 | tf_op jit(solution)/shard_map/ffn/pallas_call | solution.py:153
  508.4 5.1 all-to-all-start
  513.5 0.1 slice_bitcast_fusion.47
  513.6 0.1 slice_bitcast_fusion.39
  513.7 0.1 fusion.40
  513.8 3.6 fusion.25
  517.4 4.5 fusion.17
  521.9 4.9 fusion.1
  526.8 91.2 %all-to-all-done = bf16[8,144,4096]{2,1,0:T(8,128)(2,1)} async-done(((bf16[8,144,4096]{2,1,0:T(8,128)(2,1)}), bf16[8,144,4096]{2,1,0:T(8,128)(2,1)}, u32[]{:S(2)}, u32[]{:S(2)}) %all-to-all-start) | async-done | bytes 9437216 | tf_op jit(solution)/shard_map/all_to_all | solution.py:208
  618.0 4.9 fusion.9
  622.9 2.2 pad_maximum_fusion
  (34 shorter events, 0.3 us)
Async XLA Ops:
  6.5 44.8 %all-gather.16.cloned.1.call-start = ((), (), s32[]{:S(2)}) async-start(), calls=%async_computation.7 | async-start | bytes 7077888 | tf_op jit(solution)/shard_map/all_gather | solution.py:204
  8.7 147.6 %all-gather.14.cloned.1.call-start = ((), (), s32[]{:S(2)}) async-start(), calls=%async_computation.6 | async-start | bytes 9437184 | tf_op jit(solution)/shard_map/all_gather | solution.py:204
  11.1 260.4 %all-gather.12.cloned.1.call-start = ((), (), s32[]{:S(2)}) async-start(), calls=%async_computation.5 | async-start | bytes 10616832 | tf_op jit(solution)/shard_map/all_gather | solution.py:204
  14.5 0.7 copy-start.4
  14.5 378.0 %all-gather.10.cloned.1.call-start = ((), (), s32[]{:S(2)}) async-start(), calls=%async_computation.4 | async-start | bytes 10616832 | tf_op jit(solution)/shard_map/all_gather | solution.py:204
  31.3 0.6 copy-start.7
  31.4 0.6 copy-start.8
  32.0 3.9 copy-start
  32.0 4.9 copy-start.1
  34.4 115.4 %copy-start.9 = (s32[9]{0:T(128)}, s32[9]{0:T(128)S(1)}, u32[]{:S(2)}) copy-start(s32[9]{0:T(128)S(1)} %pad_add_fusion.1.base_ref) | copy-start | bytes 112
  34.5 115.3 %copy-start.2 = (s32[8,128]{1,0:T(8,128)}, s32[8,128]{1,0:T(8,128)S(1)}, u32[]{:S(2)}) copy-start(s32[8,128]{1,0:T(8,128)S(1)} %fusion.38.dl_ref) | copy-start | bytes 12292
  35.8 15.6 %copy-start.10 = (s32[9]{0:T(128)}, s32[9]{0:T(128)S(1)}, u32[]{:S(2)}) copy-start(s32[9]{0:T(128)S(1)} %pad_add_fusion.base_ref) | copy-start | bytes 112
  35.9 15.5 %copy-start.3 = (s32[8,96]{1,0:T(8,128)}, s32[8,96]{1,0:T(8,128)S(1)}, u32[]{:S(2)}) copy-start(s32[8,96]{1,0:T(8,128)S(1)} %fusion.37.dl_ref) | copy-start | bytes 9220
  149.8 115.6 %all-to-all-start.3 = ((bf16[8,96,4096]{2,1,0:T(8,128)(2,1)}), bf16[8,96,4096]{2,1,0:T(8,128)(2,1)}, u32[]{:S(2)}, u32[]{:S(2)}) async-start(bf16[8,96,4096]{2,1,0:T(8,128)(2,1)} %bitcast.232), calls=%async_computation.3 | async-start | bytes 12582912 | tf_op jit(solution)/shard_map/all_to_all | solution.py:208
  265.4 121.7 %all-to-all-start.2 = ((bf16[8,128,4096]{2,1,0:T(8,128)(2,1)}), bf16[8,128,4096]{2,1,0:T(8,128)(2,1)}, u32[]{:S(2)}, u32[]{:S(2)}) async-start(bf16[8,128,4096]{2,1,0:T(8,128)(2,1)} %bitcast.231), calls=%async_computation.2 | async-start | bytes 16777216 | tf_op jit(solution)/shard_map/all_to_all | solution.py:208
  387.1 121.2 %all-to-all-start.1 = ((bf16[8,144,4096]{2,1,0:T(8,128)(2,1)}), bf16[8,144,4096]{2,1,0:T(8,128)(2,1)}, u32[]{:S(2)}, u32[]{:S(2)}) async-start(bf16[8,144,4096]{2,1,0:T(8,128)(2,1)} %bitcast.230), calls=%async_computation.1 | async-start | bytes 18874368 | tf_op jit(solution)/shard_map/all_to_all | solution.py:208
  508.4 5.2 copy-start.5
  508.4 5.2 copy-start.6
  508.4 109.7 %all-to-all-start = ((bf16[8,144,4096]{2,1,0:T(8,128)(2,1)}), bf16[8,144,4096]{2,1,0:T(8,128)(2,1)}, u32[]{:S(2)}, u32[]{:S(2)}) async-start(bf16[8,144,4096]{2,1,0:T(8,128)(2,1)} %bitcast.229), calls=%async_computation | async-start | bytes 18874368 | tf_op jit(solution)/shard_map/all_to_all | solution.py:208
Sparse Core Ops, SparseCore 0:
  8.9 42.3 all-gather.15
  53.0 46.5 all-gather.13
  101.2 51.1 all-gather.11
  153.8 96.1 all-gather.9
